TPU v7x, 32 devices: a whole 2x2x4 slice. The times are simulated.
32 devices in a mesh: fsdp: 4 (over y, x), seq: 8 (over z, core).
Axes of the slice: x: 2, y: 2, z: 4, core: 2. Of those that a mesh axis runs over, the one named last changes fastest.
Arguments:
- image_input: bfloat16 [4, 1024, 1536], P('fsdp', 'seq'), may hold values from -6 to 6
- text_input: bfloat16 [4, 128, 1536], P('fsdp'), may hold values from -6 to 6
- w_qkv: bfloat16 [1536, 3, 2048], P('fsdp'), may hold values from -0.15625 to 0.15625
- query_gain: float32 [128], replicated, may hold values from 1.2 to 2.4
- key_gain: float32 [128], replicated, may hold values from 1.2 to 2.4
- image_cotangent: bfloat16 [4, 1024, 2048], P('fsdp', 'seq'), may hold values from -6 to 6
- text_cotangent: bfloat16 [4, 128, 2048], P('fsdp'), may hold values from -6 to 6
Outputs:
- image_grad: bfloat16 [4, 1024, 1536], P('fsdp', 'seq')
- text_grad: bfloat16 [4, 128, 1536], P('fsdp')
- weight_grad: float32 [1536, 3, 2048], P('fsdp', None, 'seq')
- gain_grad: float32 [2, 128], replicated
All inputs are finite; a program needn't handle non-finite values.
Results may differ from a plain program's by a relative error of at most 0.018.
The roundings to bfloat16 on the way count: a program that leaves them out, or rounds other values in their place, can miss the bound.
Values may be sent and summed in bfloat16 or wider, within the bound.
A program may use at most 192 MiB of HBM per device.

v0:
```python
import math
import jax
import jax.numpy as jnp
from jax import lax
from jax.sharding import PartitionSpec as P

HEADS = 16
HEAD = 128
epsilon = 1e-06
query_parts = 4


def rms_forward(values, gain):
    floated = values.astype(jnp.float32)
    inverse = lax.rsqrt(jnp.mean(floated * floated, axis=-1, keepdims=True) + epsilon)
    return (floated, inverse, (floated * inverse * gain).astype(jnp.bfloat16))


def rms_backward(floated, inverse, gain, incoming):
    weighted = incoming * gain
    inner_mean = jnp.mean(weighted * floated, axis=-1, keepdims=True)
    grad_input = inverse * weighted - floated * inverse * inverse * inverse * inner_mean
    grad_gain = jnp.sum(incoming * floated * inverse, axis=0)
    return (grad_input, grad_gain)


def head_backward(query_rows, key_rows, value_rows, incoming, query_gain, key_gain):
    query_float, query_inverse, query_normed = rms_forward(query_rows, query_gain)
    key_float, key_inverse, key_normed = rms_forward(key_rows, key_gain)
    length = query_rows.shape[0]
    width = query_rows.shape[1]
    block_rows = length // query_parts
    factor = 1.0 / math.sqrt(width)
    query_blocks = query_normed.reshape(query_parts, block_rows, width)
    incoming_blocks = incoming.reshape(query_parts, block_rows, width)

    def visit(carried, pieces):
        key_total, value_total = carried
        query_piece, incoming_piece = pieces
        scores = jnp.dot(query_piece, key_normed.T, preferred_element_type=jnp.float32) * factor
        attention = jax.nn.softmax(scores, axis=-1)
        attention_grad = jnp.dot(incoming_piece, value_rows.T, preferred_element_type=jnp.float32)
        row_dot = jnp.sum(attention * attention_grad, axis=-1, keepdims=True)
        score_grad = (attention * (attention_grad - row_dot)).astype(jnp.bfloat16)
        value_total = value_total + jnp.dot(
            attention.astype(jnp.bfloat16).T, incoming_piece, preferred_element_type=jnp.float32
        )
        key_total = (
            key_total
            + jnp.dot(score_grad.T, query_piece, preferred_element_type=jnp.float32) * factor
        )
        query_grad = jnp.dot(score_grad, key_normed, preferred_element_type=jnp.float32) * factor
        return ((key_total, value_total), query_grad)

    zeros_init = jnp.zeros((length, width), jnp.float32)
    (key_total, value_total), query_pieces = lax.scan(
        visit, (zeros_init, zeros_init), (query_blocks, incoming_blocks)
    )
    query_grad = query_pieces.reshape(length, width)
    query_input_grad, query_gain_grad = rms_backward(
        query_float, query_inverse, query_gain, query_grad
    )
    key_input_grad, key_gain_grad = rms_backward(key_float, key_inverse, key_gain, key_total)
    stacked = jnp.stack([query_input_grad, key_input_grad, value_total], axis=1).astype(
        jnp.bfloat16
    )
    return (stacked, jnp.stack([query_gain_grad, key_gain_grad], axis=0))


def local(image_input, text_input, w_qkv, query_gain, key_gain, image_cotangent, text_cotangent):
    member_count = lax.axis_size("seq")
    own_index = lax.axis_index("seq")
    local_heads = HEADS // member_count
    own_width = local_heads * HEAD
    offset = own_index * own_width
    text_length = text_input.shape[1]
    image_rows_dev = image_input.shape[1]
    weights = lax.all_gather(w_qkv, "fsdp", axis=0, tiled=True)
    image_triple = jnp.einsum(
        "btd,dch->btch", image_input, weights, preferred_element_type=jnp.float32
    ).astype(jnp.bfloat16)
    stacked = jnp.concatenate([image_triple, image_cotangent[:, :, None, :]], axis=2)
    arrived = lax.all_to_all(stacked, "seq", split_axis=3, concat_axis=1, tiled=True)
    own_weights = lax.dynamic_slice_in_dim(weights, offset, own_width, 2)
    text_triple = jnp.einsum(
        "btd,dch->btch", text_input, own_weights, preferred_element_type=jnp.float32
    ).astype(jnp.bfloat16)
    text_incoming = lax.dynamic_slice_in_dim(text_cotangent, offset, own_width, 2)
    joined_triple = jnp.concatenate([text_triple, arrived[:, :, :3]], axis=1)
    joined_incoming = jnp.concatenate([text_incoming, arrived[:, :, 3]], axis=1)
    batch_rows = joined_triple.shape[0]
    length = joined_triple.shape[1]
    split_triple = joined_triple.reshape(batch_rows, length, 3, local_heads, HEAD)
    split_incoming = joined_incoming.reshape(batch_rows, length, local_heads, HEAD)
    per_head = jax.vmap(head_backward, in_axes=(1, 1, 1, 1, None, None), out_axes=(2, 0))
    per_batch = jax.vmap(per_head, in_axes=(0, 0, 0, 0, None, None), out_axes=(0, 0))
    head_grads, gain_parts = per_batch(
        split_triple[:, :, 0],
        split_triple[:, :, 1],
        split_triple[:, :, 2],
        split_incoming,
        query_gain,
        key_gain,
    )
    head_grads = head_grads.reshape(batch_rows, length, 3, own_width)
    text_grads = head_grads[:, :text_length]
    image_grads = head_grads[:, text_length:]
    gain_total = lax.psum(jnp.sum(gain_parts, axis=(0, 1)), ("fsdp", "seq"))
    image_tokens = lax.all_to_all(image_grads, "seq", split_axis=1, concat_axis=3, tiled=True)
    text_partial = jnp.einsum(
        "btch,dch->btd", text_grads, own_weights, preferred_element_type=jnp.float32
    )
    text_out = lax.psum(text_partial.astype(jnp.bfloat16), "seq")
    image_out = jnp.einsum(
        "btch,dch->btd", image_tokens, weights, preferred_element_type=jnp.float32
    ).astype(jnp.bfloat16)
    text_part = jnp.einsum(
        "btd,btch->dch", text_input, text_grads, preferred_element_type=jnp.float32
    )
    whole_image = lax.all_gather(image_input, "seq", axis=1, tiled=True)

    def add_block(block, running):
        start = (block * image_rows_dev).astype(jnp.int32)
        image_block = lax.dynamic_slice_in_dim(whole_image, start, image_rows_dev, 1)
        grad_block = lax.dynamic_slice_in_dim(image_grads, start, image_rows_dev, 1)
        selected = (block == own_index).astype(jnp.float32)
        term = (
            jnp.einsum("btd,btch->dch", image_block, grad_block, preferred_element_type=jnp.float32)
            + text_part * selected
        )
        rounded = lax.optimization_barrier(term.astype(jnp.bfloat16))
        return running + rounded.astype(jnp.float32)

    start_total = jnp.zeros((image_input.shape[2], 3, own_width), jnp.float32)
    head_total = lax.fori_loop(0, member_count, add_block, start_total)
    grad_weights = lax.psum_scatter(
        head_total.astype(jnp.bfloat16), "fsdp", scatter_dimension=0, tiled=True
    ).astype(jnp.float32)
    return (image_out, text_out, grad_weights, gain_total)


def solution(mesh):
    return jax.shard_map(
        local,
        mesh=mesh,
        in_specs=(
            P("fsdp", "seq", None),
            P("fsdp", None, None),
            P("fsdp", None, None),
            P(),
            P(),
            P("fsdp", "seq", None),
            P("fsdp", None, None),
        ),
        out_specs=(P("fsdp", "seq", None), P("fsdp", None, None), P("fsdp", None, "seq"), P()),
        check_vma=False,
    )
```

profile of v0, /device:TPU:0, one launch (start us, length us, event | category | flops | bytes accessed | tf_op | source)
XLA Modules:
  0.0 548.0 jit_solution(7560957821269184910)
XLA Ops:
  8.1 6.7 %copy.122 = bf16[384,3,2048]{0,2,1:T(8,128)(2,1)} copy(bf16[384,3,2048]{2,0,1:T(8,128)(2,1)} %param.13) | data formatting | bytes 9437184 | tf_op args[2]
  14.8 178.5 %all-gather.3.cloned.1.call-done = bf16[1536,3,2048]{0,2,1:T(8,128)(2,1)} async-done(((bf16[384,3,2048]{0,2,1:T(8,128)(2,1)}), bf16[1536,3,2048]{0,2,1:T(8,128)(2,1)}) %all-gather.3.cloned.1.call-update) | async-done | bytes 18874384 | tf_op jit(solution)/shard_map/all_gather | solution.py:78
  193.3 13.7 %fusion.44 = bf16[1,128,3,2048]{3,1,2,0:T(8,128)(2,1)} fusion(bf16[1536,3,2048]{0,2,1:T(8,128)(2,1)} %all-gather.3.cloned.1.call-done, bf16[1,128,1536]{2,1,0:T(8,128)(2,1)S(1)} %copy-done.16), kind=kOutput, calls=%fused_computation.46 | convolution fusion | flops 2416705536 | bytes 20840448 | tf_op jit(solution)/shard_map/btd,dch->btch/dot_general | solution.py:79
  208.6 2.6 copy.124
  211.2 4.6 all-to-all-start
  220.7 69.4 %all-to-all-done = bf16[1,128,4,2048]{1,2,0,3:T(4,128)(2,1)S(1)} async-done(((bf16[1,128,4,2048]{1,2,0,3:T(4,128)(2,1)}), bf16[1,128,4,2048]{1,2,0,3:T(4,128)(2,1)S(1)}, u32[]{:S(2)}, u32[]{:S(2)}) %all-to-all-start) | async-done | bytes 2097184 | tf_op jit(solution)/shard_map/all_to_all | solution.py:83
  291.8 2.9 copy.126
  302.9 52.1 %while.29 = (s32[]{:T(128)}, f32[1,2,1152,128]{3,2,1,0:T(8,128)}, f32[1,2,1152,128]{3,2,1,0:T(8,128)}, f32[4,1,2,288,128]{4,3,0,2,1:T(8,128)}, bf16[4,1,2,288,12...) while((s32[]{:T(128)}, f32[1,2,1152,128]{3,2,1,0:T(8,128)}, ...), condition=%wide.region_6.7_spmd.clone, body=%wide.region_2.6_spmd.clone.sunk | while | flops 858858048 | bytes 69760840 | solution.py:56
  364.4 2.9 convolution_bitcast_fusion.1
  367.3 6.0 %copy.146 = f32[1536,3,256]{2,0,1:T(8,128)} copy(f32[1536,3,256]{0,2,1:T(8,128)} %convolution_bitcast_fusion.1) | data formatting | bytes 9437184
  373.4 64.9 %while.30 = (s32[]{:T(128)}, f32[1536,3,256]{2,0,1:T(8,128)}, bf16[1,1024,1536]{1,2,0:T(8,128)(2,1)}, bf16[1,1024,3,256]{1,3,2,0:T(8,128)(2,1)}, s32[]{:T(128)},...) while((s32[]{:T(128)}, f32[1536,3,256]{2,0,1:T(8,128)}, ...), condition=%wide.region_11.12_spmd.clone, body=%wide.region_10.11_spmd.clone.sunk | while | flops 309067776 | bytes 19465908 | solution.py:135
  373.4 3.4 add_convert_fusion.2
  376.7 2.7 select_add_fusion.2
  379.4 3.4 add_convert_fusion.2
  382.8 5.0 select_add_fusion.2
  387.8 3.4 add_convert_fusion.2
  391.2 5.0 select_add_fusion.2
  396.3 3.4 add_convert_fusion.2
  399.6 5.0 select_add_fusion.2
  404.7 3.4 add_convert_fusion.2
  408.0 5.0 select_add_fusion.2
  413.1 3.4 add_convert_fusion.2
  416.4 5.0 select_add_fusion.2
  421.5 3.4 add_convert_fusion.2
  424.8 5.0 select_add_fusion.2
  429.9 3.4 add_convert_fusion.2
  433.3 5.0 select_add_fusion.2
  438.3 4.0 convert_element_type.125
  446.3 3.6 all-to-all-start.1
  449.9 3.0 fusion.47
  453.0 68.9 %psum.15 = f32[2,128]{1,0:T(2,128)} all-reduce(f32[2,128]{1,0:T(2,128)S(1)} %maximum_reduce_fusion), channel_id=1, replica_groups=mesh['fsdp'=4,'seq'=8] {'fsdp','seq'}, use_global_device_ids=true, to_apply=%region_16.17 | all-reduce | flops 256 | bytes 2048 | tf_op jit(solution)/shard_map/psum | solution.py:108
  526.9 9.8 %fusion.48 = bf16[1,128,1536]{2,1,0:T(8,128)(2,1)} fusion(bf16[128,3,2048]{2,0,1:T(8,128)(2,1)S(1)} %reshape.317, bf16[1536,3,2048]{0,2,1:T(8,128)(2,1)} %all-gather.3.cloned.1.call-done), kind=kOutput, calls=%fused_computation.54 | convolution fusion | flops 2416115712 | bytes 20840448 | tf_op jit(solution)/shard_map/btch,dch->btd/dot_general | solution.py:114
  (164 shorter events, 90.1 us)
Async XLA Ops:
  8.0 210.1 %copy-start = (bf16[1,128,2048]{2,1,0:T(8,128)(2,1)S(1)}, bf16[1,128,2048]{2,1,0:T(8,128)(2,1)}, u32[]{:S(2)}) copy-start(bf16[1,128,2048]{2,1,0:T(8,128)(2,1)} %param.17) | copy-start | bytes 1572868
  8.0 185.3 %all-gather.3.cloned.1.call-start = ((), (), s32[]{:S(2)}) async-start(), calls=%async_computation.3 | async-start | bytes 23592960 | tf_op jit(solution)/shard_map/all_gather | solution.py:78
  14.7 178.6 %copy-start.16 = (bf16[1,128,1536]{2,1,0:T(8,128)(2,1)S(1)}, bf16[1,128,1536]{2,1,0:T(8,128)(2,1)}, u32[]{:S(2)}) copy-start(bf16[1,128,1536]{2,1,0:T(8,128)(2,1)} %param.11) | copy-start | bytes 1179652
  14.8 192.3 %copy-start.20 = (bf16[1,128,2048]{2,1,0:T(8,128)(2,1)S(1)}, bf16[1,128,2048]{2,1,0:T(8,128)(2,1)}, u32[]{:S(2)}) copy-start(bf16[1,128,2048]{2,1,0:T(8,128)(2,1)} %param.16) | copy-start | bytes 1572868
  211.2 78.9 %all-to-all-start = ((bf16[1,128,4,2048]{1,2,0,3:T(4,128)(2,1)}), bf16[1,128,4,2048]{1,2,0,3:T(4,128)(2,1)S(1)}, u32[]{:S(2)}, u32[]{:S(2)}) async-start(bf16[1,128,4,2048]{1,2,0,3:T(4,128)(2,1)} %copy.124), calls=%async_computation | async-start | bytes 4194304 | tf_op jit(solution)/shard_map/all_to_all | solution.py:83
  215.8 2.5 copy-start.14
  215.8 157.6 %all-gather.5.cloned.1.call-start = ((), (), s32[]{:S(2)}) async-start(), calls=%async_computation.5 | async-start | bytes 3538944 | tf_op jit(solution)/shard_map/all_gather | solution.py:120
  217.9 318.8 %reduce-scatter.2.cloned.1.call-start = ((), (), s32[]{:S(2)}) async-start(), calls=%async_computation.6 | async-start | bytes 2949120 | tf_op jit(solution)/shard_map/reduce_scatter | solution.py:136
  305.1 2.4 copy-start.2
  309.8 2.3 copy-start.3
  309.8 2.3 copy-start.17
  312.0 2.6 copy-start.5
  312.1 2.6 copy-start.19
  318.1 2.4 copy-start.2
  322.8 2.3 copy-start.3
  322.8 2.3 copy-start.17
  325.1 2.6 copy-start.5
  325.1 2.6 copy-start.19
  331.2 2.4 copy-start.2
  335.8 2.3 copy-start.3
  335.8 2.3 copy-start.17
  338.1 2.6 copy-start.5
  338.1 2.6 copy-start.19
  344.2 2.4 copy-start.2
  348.8 2.3 copy-start.3
  348.9 2.3 copy-start.17
  351.1 2.6 copy-start.5
  351.2 2.6 copy-start.19
  355.0 2.4 copy-start.6
  446.3 75.7 %all-to-all-start.1 = ((bf16[1,1024,3,256]{3,2,0,1:T(4,128)(2,1)}), bf16[1,1024,3,256]{3,2,0,1:T(4,128)(2,1)S(1)}, u32[]{:S(2)}, u32[]{:S(2)}) async-start(bf16[1,1024,3,256]{3,2,0,1:T(4,128)(2,1)} %copy.140), calls=%async_computation.1 | async-start | bytes 4194304 | tf_op jit(solution)/shard_map/all_to_all | solution.py:109
  449.9 88.9 %all-reduce.2.cloned.1.call-start = ((), (), s32[]{:S(2)}) async-start(), calls=%async_computation.4 | async-start | bytes 786432 | tf_op jit(solution)/shard_map/psum | solution.py:113
  526.8 13.7 %copy-start.1 = (bf16[1,128,2048]{2,1,0:T(8,128)(2,1)S(1)}, bf16[1,128,2048]{2,1,0:T(8,128)(2,1)}, u32[]{:S(2)}) copy-start(bf16[1,128,2048]{2,1,0:T(8,128)(2,1)} %param.17) | copy-start | bytes 1572868
  (18 other events, 27.3 us)
Sparse Core Ops, SparseCore 0:
  14.9 178.3 all-gather.2
  442.5 35.8 reduce-scatter.1
Sparse Core Ops, SparseCore 1:
  218.5 70.8 all-gather.4
  453.3 69.3 all-reduce.1
where the time goes:
time: 550 us; the launch traced here: 548 us
  waiting for transfers between devices  248 us (45%)
  matrix products  101 us (18%)
  blocking collectives  68.9 us (13%)
  other arithmetic  58.1 us (11%)
  local copies, waits for them, and re-layouts  46.7 us (8%)
  between operations  15.8 us (3%)
  starting transfers between devices  8.54 us (2%)
    all_gather x1, waiting for transfers between devices, local(): weights = lax.all_gather(w_qkv, 'fsdp', axis=0, tiled=True)  179 us
    all_to_all x1, waiting for transfers between devices, local(): lax.all_to_all(stacked, 'seq', split_axis=3, concat_axis=1, tiled=True)  69.4 us
    psum x1, blocking collectives, local(): gain_total = lax.psum(jnp.sum(gain_parts, axis=(0, 1)), ('fsdp', 'seq'))  68.9 us
    add x8, other arithmetic, add_block(): return running + rounded.astype(jnp.float32)  37.9 us
    dot_general x8, matrix products, add_block(): jnp.einsum('btd,btch->dch', image_block, grad_block, preferred_element_ty...  26.9 us
    unnamed x37, local copies, waits for them, and re-layouts  20.7 us
    dot_general x1, matrix products, local(): jnp.einsum('btd,dch->btch', image_input, weights, preferred_element_type=...  13.7 us
  transfers between devices with their start and end apart: 6, of which 2 were waited for; matrix products, arithmetic and copies ran while one was open for 20% of the time, Pallas kernels for 0%

commit v1 on v0

--- a/solution.py
+++ b/solution.py
@@ -105,7 +105,7 @@
     head_grads = head_grads.reshape(batch_rows, length, 3, own_width)
     text_grads = head_grads[:, :text_length]
     image_grads = head_grads[:, text_length:]
-    gain_total = lax.psum(jnp.sum(gain_parts, axis=(0, 1)), ("fsdp", "seq"))
+    gain_total = lax.psum(lax.psum(jnp.sum(gain_parts, axis=(0, 1)), "seq"), "fsdp")
     image_tokens = lax.all_to_all(image_grads, "seq", split_axis=1, concat_axis=3, tiled=True)
     text_partial = jnp.einsum(
         "btch,dch->btd", text_grads, own_weights, preferred_element_type=jnp.float32

time: 550 us -> 544 us (0.989); the launches traced: 548 us -> 536 us
  blocking collectives: 68.9 us -> 56.4 us
    psum x1 -> x2, blocking collectives: 68.9 us -> 56.4 us  [the longest x1 47 us: local(): lax.psum(jnp.sum(gain_parts, axis=(0, 1)), 'seq')]
where the time goes in v1:
time: 544 us; the launch traced here: 536 us
  waiting for transfers between devices  248 us (46%)
  matrix products  101 us (19%)
  other arithmetic  58.1 us (11%)
  blocking collectives  56.4 us (10%)
  local copies, waits for them, and re-layouts  46.7 us (9%)
  between operations  15.8 us (3%)
  starting transfers between devices  8.54 us (2%)
    all_gather x1, waiting for transfers between devices, local(): weights = lax.all_gather(w_qkv, 'fsdp', axis=0, tiled=True)  179 us
    all_to_all x1, waiting for transfers between devices, local(): lax.all_to_all(stacked, 'seq', split_axis=3, concat_axis=1, tiled=True)  69.4 us
    psum x1, blocking collectives, local(): lax.psum(jnp.sum(gain_parts, axis=(0, 1)), 'seq')  47 us
    add x8, other arithmetic, add_block(): return running + rounded.astype(jnp.float32)  37.9 us
    dot_general x8, matrix products, add_block(): jnp.einsum('btd,btch->dch', image_block, grad_block, preferred_element_ty...  26.9 us
    unnamed x37, local copies, waits for them, and re-layouts  20.7 us
    dot_general x1, matrix products, local(): jnp.einsum('btd,dch->btch', image_input, weights, preferred_element_type=...  13.7 us
  transfers between devices with their start and end apart: 6, of which 2 were waited for; matrix products, arithmetic and copies ran while one was open for 20% of the time, Pallas kernels for 0%

profile of v1, /device:TPU:0, one launch (start us, length us, event | category | flops | bytes accessed | tf_op | source)
XLA Modules:
  0.0 535.5 jit_solution(6335178724556667758)
XLA Ops:
  8.1 6.7 %copy.122 = bf16[384,3,2048]{0,2,1:T(8,128)(2,1)} copy(bf16[384,3,2048]{2,0,1:T(8,128)(2,1)} %param.13) | data formatting | bytes 9437184 | tf_op args[2]
  14.8 178.5 %all-gather.3.cloned.1.call-done = bf16[1536,3,2048]{0,2,1:T(8,128)(2,1)} async-done(((bf16[384,3,2048]{0,2,1:T(8,128)(2,1)}), bf16[1536,3,2048]{0,2,1:T(8,128)(2,1)}) %all-gather.3.cloned.1.call-update) | async-done | bytes 18874384 | tf_op jit(solution)/shard_map/all_gather | solution.py:78
  193.3 13.7 %fusion.44 = bf16[1,128,3,2048]{3,1,2,0:T(8,128)(2,1)} fusion(bf16[1536,3,2048]{0,2,1:T(8,128)(2,1)} %all-gather.3.cloned.1.call-done, bf16[1,128,1536]{2,1,0:T(8,128)(2,1)S(1)} %copy-done.16), kind=kOutput, calls=%fused_computation.46 | convolution fusion | flops 2416705536 | bytes 20840448 | tf_op jit(solution)/shard_map/btd,dch->btch/dot_general | solution.py:79
  211.2 4.6 all-to-all-start
  220.8 69.4 %all-to-all-done = bf16[1,128,4,2048]{1,2,0,3:T(4,128)(2,1)S(1)} async-done(((bf16[1,128,4,2048]{1,2,0,3:T(4,128)(2,1)}), bf16[1,128,4,2048]{1,2,0,3:T(4,128)(2,1)S(1)}, u32[]{:S(2)}, u32[]{:S(2)}) %all-to-all-start) | async-done | bytes 2097184 | tf_op jit(solution)/shard_map/all_to_all | solution.py:83
  291.8 2.9 copy.126
  302.9 52.1 %while.29 = (s32[]{:T(128)}, f32[1,2,1152,128]{3,2,1,0:T(8,128)}, f32[1,2,1152,128]{3,2,1,0:T(8,128)}, f32[4,1,2,288,128]{4,3,0,2,1:T(8,128)}, bf16[4,1,2,288,12...) while((s32[]{:T(128)}, f32[1,2,1152,128]{3,2,1,0:T(8,128)}, ...), condition=%wide.region_6.7_spmd.clone, body=%wide.region_2.6_spmd.clone.sunk | while | flops 858858048 | bytes 69760840 | solution.py:56
  364.5 2.9 convolution_bitcast_fusion.1
  367.4 6.0 %copy.146 = f32[1536,3,256]{2,0,1:T(8,128)} copy(f32[1536,3,256]{0,2,1:T(8,128)} %convolution_bitcast_fusion.1) | data formatting | bytes 9437184
  373.4 64.8 %while.30 = (s32[]{:T(128)}, f32[1536,3,256]{2,0,1:T(8,128)}, bf16[1,1024,1536]{1,2,0:T(8,128)(2,1)}, bf16[1,1024,3,256]{1,3,2,0:T(8,128)(2,1)}, s32[]{:T(128)},...) while((s32[]{:T(128)}, f32[1536,3,256]{2,0,1:T(8,128)}, ...), condition=%wide.region_11.12_spmd.clone, body=%wide.region_10.11_spmd.clone.sunk | while | flops 309067776 | bytes 19465908 | solution.py:135
  373.4 3.4 add_convert_fusion.2
  376.8 2.7 select_add_fusion.2
  379.5 3.4 add_convert_fusion.2
  382.8 5.0 select_add_fusion.2
  387.9 3.4 add_convert_fusion.2
  391.2 5.0 select_add_fusion.2
  396.3 3.4 add_convert_fusion.2
  399.6 5.0 select_add_fusion.2
  404.7 3.4 add_convert_fusion.2
  408.0 5.0 select_add_fusion.2
  413.1 3.4 add_convert_fusion.2
  416.4 5.0 select_add_fusion.2
  421.5 3.4 add_convert_fusion.2
  424.8 5.0 select_add_fusion.2
  429.8 3.4 add_convert_fusion.2
  433.2 5.0 select_add_fusion.2
  438.2 4.0 convert_element_type.125
  446.2 3.6 all-to-all-start.1
  449.9 3.0 fusion.47
  453.0 47.0 %psum.22 = f32[2,128]{1,0:T(2,128)S(1)} all-reduce(f32[2,128]{1,0:T(2,128)S(1)} %maximum_reduce_fusion), channel_id=1, replica_groups=mesh['fsdp'=4,'seq'=8] {'seq'}, use_global_device_ids=true, to_apply=%region_16.17 | all-reduce | flops 256 | bytes 2048 | tf_op jit(solution)/shard_map/psum | solution.py:108
  500.0 9.5 %psum.23 = f32[2,128]{1,0:T(2,128)} all-reduce(f32[2,128]{1,0:T(2,128)S(1)} %psum.22), channel_id=1, replica_groups=mesh['fsdp'=4,'seq'=8] {'fsdp'}, use_global_device_ids=true, to_apply=%region_17.18 | all-reduce | flops 256 | bytes 2048 | tf_op jit(solution)/shard_map/psum | solution.py:108
  514.4 9.8 %fusion.48 = bf16[1,128,1536]{2,1,0:T(8,128)(2,1)} fusion(bf16[128,3,2048]{2,0,1:T(8,128)(2,1)S(1)} %reshape.317, bf16[1536,3,2048]{0,2,1:T(8,128)(2,1)} %all-gather.3.cloned.1.call-done), kind=kOutput, calls=%fused_computation.54 | convolution fusion | flops 2416115712 | bytes 20840448 | tf_op jit(solution)/shard_map/btch,dch->btd/dot_general | solution.py:114
  (165 shorter events, 92.7 us)
Async XLA Ops:
  8.0 210.1 %copy-start = (bf16[1,128,2048]{2,1,0:T(8,128)(2,1)S(1)}, bf16[1,128,2048]{2,1,0:T(8,128)(2,1)}, u32[]{:S(2)}) copy-start(bf16[1,128,2048]{2,1,0:T(8,128)(2,1)} %param.17) | copy-start | bytes 1572868
  8.0 185.3 %all-gather.3.cloned.1.call-start = ((), (), s32[]{:S(2)}) async-start(), calls=%async_computation.3 | async-start | bytes 23592960 | tf_op jit(solution)/shard_map/all_gather | solution.py:78
  14.7 178.6 %copy-start.16 = (bf16[1,128,1536]{2,1,0:T(8,128)(2,1)S(1)}, bf16[1,128,1536]{2,1,0:T(8,128)(2,1)}, u32[]{:S(2)}) copy-start(bf16[1,128,1536]{2,1,0:T(8,128)(2,1)} %param.11) | copy-start | bytes 1179652
  14.8 192.3 %copy-start.20 = (bf16[1,128,2048]{2,1,0:T(8,128)(2,1)S(1)}, bf16[1,128,2048]{2,1,0:T(8,128)(2,1)}, u32[]{:S(2)}) copy-start(bf16[1,128,2048]{2,1,0:T(8,128)(2,1)} %param.16) | copy-start | bytes 1572868
  211.2 78.9 %all-to-all-start = ((bf16[1,128,4,2048]{1,2,0,3:T(4,128)(2,1)}), bf16[1,128,4,2048]{1,2,0,3:T(4,128)(2,1)S(1)}, u32[]{:S(2)}, u32[]{:S(2)}) async-start(bf16[1,128,4,2048]{1,2,0,3:T(4,128)(2,1)} %copy.124), calls=%async_computation | async-start | bytes 4194304 | tf_op jit(solution)/shard_map/all_to_all | solution.py:83
  215.8 2.5 copy-start.14
  215.8 157.6 %all-gather.5.cloned.1.call-start = ((), (), s32[]{:S(2)}) async-start(), calls=%async_computation.5 | async-start | bytes 3538944 | tf_op jit(solution)/shard_map/all_gather | solution.py:120
  217.9 306.3 %reduce-scatter.2.cloned.1.call-start = ((), (), s32[]{:S(2)}) async-start(), calls=%async_computation.6 | async-start | bytes 2949120 | tf_op jit(solution)/shard_map/reduce_scatter | solution.py:136
  305.1 2.4 copy-start.2
  309.8 2.3 copy-start.3
  309.8 2.3 copy-start.17
  312.0 2.6 copy-start.5
  312.1 2.6 copy-start.19
  318.1 2.4 copy-start.2
  322.8 2.3 copy-start.3
  322.8 2.3 copy-start.17
  325.1 2.6 copy-start.5
  325.1 2.6 copy-start.19
  331.2 2.4 copy-start.2
  335.8 2.3 copy-start.3
  335.8 2.3 copy-start.17
  338.1 2.6 copy-start.5
  338.1 2.6 copy-start.19
  344.2 2.4 copy-start.2
  348.9 2.3 copy-start.3
  348.9 2.3 copy-start.17
  351.1 2.6 copy-start.5
  351.2 2.6 copy-start.19
  355.0 2.4 copy-start.6
  446.2 63.2 %all-to-all-start.1 = ((bf16[1,1024,3,256]{3,2,0,1:T(4,128)(2,1)}), bf16[1,1024,3,256]{3,2,0,1:T(4,128)(2,1)S(1)}, u32[]{:S(2)}, u32[]{:S(2)}) async-start(bf16[1,1024,3,256]{3,2,0,1:T(4,128)(2,1)} %copy.140), calls=%async_computation.1 | async-start | bytes 4194304 | tf_op jit(solution)/shard_map/all_to_all | solution.py:109
  449.9 76.5 %all-reduce.2.cloned.1.call-start = ((), (), s32[]{:S(2)}) async-start(), calls=%async_computation.4 | async-start | bytes 786432 | tf_op jit(solution)/shard_map/psum | solution.py:113
  514.3 13.8 %copy-start.1 = (bf16[1,128,2048]{2,1,0:T(8,128)(2,1)S(1)}, bf16[1,128,2048]{2,1,0:T(8,128)(2,1)}, u32[]{:S(2)}) copy-start(bf16[1,128,2048]{2,1,0:T(8,128)(2,1)} %param.17) | copy-start | bytes 1572868
  (18 other events, 27.4 us)
Sparse Core Ops, SparseCore 0:
  14.9 178.3 all-gather.2
  442.4 35.3 reduce-scatter.1
Sparse Core Ops, SparseCore 1:
  218.5 70.8 all-gather.4
  453.2 67.3 all-reduce.1
